TPU v7x, 32 devices: a whole 2x2x4 slice. The times are simulated.
32 devices in a mesh: seq: 8 (over z, y), batch: 4 (over x, core).
Axes of the slice: x: 2, y: 2, z: 4, core: 2. Of those that a mesh axis runs over, the one named last changes fastest.
Arguments:
- queries: bfloat16 [4, 4096, 16, 128], P('batch', 'seq'), may hold values from -5 to 5
- keys: bfloat16 [4, 4096, 16, 128], P('batch', 'seq'), may hold values from -5 to 5
- values: bfloat16 [4, 4096, 16, 128], P('batch', 'seq'), may hold values from -5 to 5
- keep_count: int32 [4, 16, 32], P('batch'), may hold values from 0 to 128
- query_map: bfloat16 [16, 128, 8], replicated, may hold values from -0.5 to 0.5
- key_map: bfloat16 [16, 128, 8], replicated, may hold values from -0.5 to 0.5
- cotangent: bfloat16 [4, 4096, 16, 128], P('batch', 'seq'), may hold values from -5 to 5
Outputs:
- attended: bfloat16 [4, 4096, 16, 128], P('batch', 'seq')
- grad_query_map: float32 [16, 128, 8], replicated
- grad_key_map: float32 [16, 128, 8], replicated
All inputs are finite; a program needn't handle non-finite values.
Results may differ from a plain program's by a relative error of at most 0.0035.
Values may be sent and summed in bfloat16 or wider, within the bound.
A program may use at most 128 MiB of HBM per device.

v0:
```python
import math
import jax
import jax.numpy as jnp
from jax import lax
from jax.sharding import PartitionSpec as P

TILE = 128
WINDOW = 256
HIGHEST = lax.Precision.HIGHEST
feature_shift = 1.5


def passed_along(value, axis, steps):
    count = lax.axis_size(axis)
    first, last = (max(0, -steps), min(count, count - steps))
    return lax.ppermute(value, axis, [(source, source + steps) for source in range(first, last)])


def prefix(shard, axis, combine, identity, reverse):
    peers, position = (lax.axis_size(axis), lax.axis_index(axis))
    everything = jax.tree.map(lambda part: lax.all_gather(part, axis), shard)
    start = jax.tree.map(
        lambda part, zero: jnp.broadcast_to(jnp.asarray(zero, part.dtype), part.shape),
        shard,
        identity,
    )

    def step(k, before):
        at = peers - 1 - k if reverse else k
        reached = at > position if reverse else at < position
        new = combine(before, jax.tree.map(lambda part: part[at], everything))
        return jax.tree.map(lambda a, b: jnp.where(reached, a, b), new, before)

    return lax.fori_loop(0, peers, step, start)


def add_pair(earlier, later):
    return (earlier[0] + later[0], earlier[1] + later[1])


def windowed(tiled, first, count, span):
    pieces = [
        lax.slice_in_dim(tiled, first + offset, first + offset + count, axis=0)
        for offset in range(span)
    ]
    return jnp.concatenate(pieces, 1)


def body(queries, keys, values, keep_count, query_map, key_map, cotangent):
    q_rows = queries[0]
    k_rows = keys[0]
    v_rows = values[0]
    cot_rows = cotangent[0].astype(jnp.float32)
    tokens, heads, width = q_rows.shape
    rank = query_map.shape[2]
    tiles_dev = tokens // TILE
    span = WINDOW // TILE
    scale = 1.0 / math.sqrt(width)
    index = lax.axis_index("seq")
    halo_rows = WINDOW - TILE
    prev_keys, prev_values = passed_along(
        (k_rows[tokens - halo_rows :], v_rows[tokens - halo_rows :]), "seq", 1
    )
    halo_tiles = halo_rows // TILE
    ext_tiles = halo_tiles + tiles_dev
    ext_rows = halo_rows + tokens
    ext_keys = jnp.concatenate([prev_keys, k_rows], 0)
    ext_values = jnp.concatenate([prev_values, v_rows], 0)
    counts = keep_count[0]
    padded_counts = jnp.concatenate([jnp.zeros((heads, tiles_dev), jnp.int32), counts], 1)
    count_start = index * tiles_dev + tiles_dev - halo_tiles
    ext_counts = lax.dynamic_slice_in_dim(padded_counts, count_start, ext_tiles, 1)
    local = jnp.arange(ext_rows, dtype=jnp.int32)
    key_pos = index * tokens - halo_rows + local
    valid = key_pos >= 0
    within = local % TILE
    kept = within[None, :] < jnp.repeat(ext_counts, TILE, axis=1)
    evicted = valid[None, :] & jnp.logical_not(kept)
    pre_q = (
        jnp.einsum("thd,hdr->thr", q_rows, query_map, preferred_element_type=jnp.float32)
        - feature_shift
    )
    pre_k = (
        jnp.einsum("thd,hdr->thr", ext_keys, key_map, preferred_element_type=jnp.float32)
        - feature_shift
    )
    feat_q = jax.nn.softplus(pre_q)
    feat_k = jax.nn.softplus(pre_k)
    valid_f = valid.astype(jnp.float32)[:, None, None]
    evict_f = evicted.T.astype(jnp.float32)[:, :, None]
    v_tiles = ext_values.astype(jnp.float32).reshape(ext_tiles, TILE, heads, width)

    def tile_state(feat):
        tiled = feat.reshape(ext_tiles, TILE, heads, rank)
        return (jnp.einsum("nthr,nthd->nhrd", tiled, v_tiles, precision=HIGHEST), jnp.sum(tiled, 1))

    all_state, all_norm = tile_state(feat_k * valid_f)
    ev_state, ev_norm = tile_state(feat_k * evict_f)
    q_tile = jnp.arange(tiles_dev, dtype=jnp.int32)[:, None] + halo_tiles
    k_tile = jnp.arange(ext_tiles, dtype=jnp.int32)[None, :]
    in_halo = (k_tile < halo_tiles).astype(jnp.float32)
    far_mix = (k_tile < q_tile - span + 1).astype(jnp.float32)
    near_mix = ((k_tile >= q_tile - span + 1) & (k_tile < q_tile)).astype(jnp.float32)
    far_coef = far_mix * (1.0 - in_halo) - near_mix * in_halo
    carried_state = jnp.sum(all_state[halo_tiles:], 0)
    carried_norm = jnp.sum(all_norm[halo_tiles:], 0)
    far_state, far_norm = prefix(
        (carried_state, carried_norm),
        "seq",
        add_pair,
        (jnp.zeros_like(carried_state), jnp.zeros_like(carried_norm)),
        False,
    )
    state = (
        far_state[None]
        + jnp.einsum("jn,nhrd->jhrd", far_coef, all_state, precision=HIGHEST)
        + jnp.einsum("jn,nhrd->jhrd", near_mix, ev_state, precision=HIGHEST)
    )
    norm = (
        far_norm[None]
        + jnp.einsum("jn,nhr->jhr", far_coef, all_norm, precision=HIGHEST)
        + jnp.einsum("jn,nhr->jhr", near_mix, ev_norm, precision=HIGHEST)
    )
    first_tile = halo_tiles - span + 1
    key_window = windowed(
        ext_keys.reshape(ext_tiles, TILE, heads, width), first_tile, tiles_dev, span
    )
    value_window = windowed(
        ext_values.reshape(ext_tiles, TILE, heads, width), first_tile, tiles_dev, span
    )
    allowed = (kept & valid[None, :]).T.reshape(ext_tiles, TILE, heads)
    allowed_window = windowed(allowed, first_tile, tiles_dev, span).transpose(0, 2, 1)
    slot = jnp.arange(span * TILE, dtype=jnp.int32)
    own_slot = slot >= (span - 1) * TILE
    causal = slot[None, :] - (span - 1) * TILE <= jnp.arange(TILE, dtype=jnp.int32)[:, None]
    live_pairs = jnp.where(
        own_slot[None, None, None, :], causal[None, None], allowed_window[:, :, None, :]
    )
    q_tiles = q_rows.reshape(tiles_dev, TILE, heads, width)
    scores = (
        jnp.einsum("nqhd,nkhd->nhqk", q_tiles, key_window, preferred_element_type=jnp.float32)
        * scale
    )
    row_max = jnp.max(jnp.where(live_pairs, scores, -jnp.inf), -1)
    weights = jnp.where(live_pairs, jnp.exp(scores - row_max[..., None]), 0.0)
    denom = jnp.sum(weights, -1).transpose(0, 2, 1).reshape(tokens, heads)
    numer = jnp.einsum(
        "nhqk,nkhd->nqhd",
        weights.astype(jnp.bfloat16),
        value_window,
        preferred_element_type=jnp.float32,
    ).reshape(tokens, heads, width)
    decay = jnp.exp(-row_max.transpose(0, 2, 1).reshape(tokens, heads))
    feat_qt = feat_q.reshape(tiles_dev, TILE, heads, rank)
    kernel_num = jnp.einsum("nthr,nhrd->nthd", feat_qt, state, precision=HIGHEST).reshape(
        tokens, heads, width
    )
    kernel_den = jnp.einsum("nthr,nhr->nth", feat_qt, norm, precision=HIGHEST).reshape(
        tokens, heads
    )
    total = denom + decay * kernel_den
    out = (numer + decay[..., None] * kernel_num) / total[..., None]
    delta = cot_rows / total[..., None]
    ratio_grad = -jnp.sum(delta * out, -1)
    grad_num = (decay[..., None] * delta).reshape(tiles_dev, TILE, heads, width)
    grad_den = (decay * ratio_grad).reshape(tiles_dev, TILE, heads)
    grad_fq = (
        jnp.einsum("nthd,nhrd->nthr", grad_num, state, precision=HIGHEST)
        + grad_den[..., None] * norm[:, None]
    )
    d_state = jnp.einsum("nthr,nthd->nhrd", feat_qt, grad_num, precision=HIGHEST)
    d_norm = jnp.einsum("nthr,nth->nhr", feat_qt, grad_den, precision=HIGHEST)
    own_state = jnp.sum(d_state, 0)
    own_norm = jnp.sum(d_norm, 0)
    after_state, after_norm = prefix(
        (own_state, own_norm),
        "seq",
        add_pair,
        (jnp.zeros_like(own_state), jnp.zeros_like(own_norm)),
        True,
    )
    own_tiles = (jnp.arange(ext_tiles, dtype=jnp.int32) >= halo_tiles).astype(jnp.float32)
    d_all = (
        jnp.einsum("jn,jhrd->nhrd", far_coef, d_state, precision=HIGHEST)
        + own_tiles[:, None, None, None] * after_state[None]
    )
    d_alln = (
        jnp.einsum("jn,jhr->nhr", far_coef, d_norm, precision=HIGHEST)
        + own_tiles[:, None, None] * after_norm[None]
    )
    d_ev = jnp.einsum("jn,jhrd->nhrd", near_mix, d_state, precision=HIGHEST)
    d_evn = jnp.einsum("jn,jhr->nhr", near_mix, d_norm, precision=HIGHEST)
    grad_all = jnp.einsum("nhrd,nthd->nthr", d_all, v_tiles, precision=HIGHEST) + d_alln[:, None]
    grad_ev = jnp.einsum("nhrd,nthd->nthr", d_ev, v_tiles, precision=HIGHEST) + d_evn[:, None]
    grad_fk = valid_f * grad_all.reshape(ext_rows, heads, rank) + evict_f * grad_ev.reshape(
        ext_rows, heads, rank
    )
    grad_pre_k = grad_fk * jax.nn.sigmoid(pre_k)
    grad_pre_q = grad_fq.reshape(tokens, heads, rank) * jax.nn.sigmoid(pre_q)
    grad_q = jnp.einsum("thd,thr->hdr", q_rows.astype(jnp.float32), grad_pre_q, precision=HIGHEST)
    grad_k = jnp.einsum("thd,thr->hdr", ext_keys.astype(jnp.float32), grad_pre_k, precision=HIGHEST)
    grad_q, grad_k = lax.psum((grad_q, grad_k), ("seq", "batch"))
    return (out.astype(jnp.bfloat16)[None], grad_q, grad_k)


def solution(mesh):
    placed = (
        P("batch", "seq", None, None),
        P("batch", "seq", None, None),
        P("batch", "seq", None, None),
        P("batch", None, None),
        P(),
        P(),
        P("batch", "seq", None, None),
    )
    return jax.shard_map(
        body,
        mesh=mesh,
        in_specs=placed,
        out_specs=(P("batch", "seq", None, None), P(), P()),
        check_vma=False,
    )
```

profile of v0, /device:TPU:0, one launch (start us, length us, event | category | flops | bytes accessed | tf_op | source)
XLA Modules:
  0.0 420.2 jit_solution(9056168187303462686)
XLA Ops:
  7.2 2.3 copy.332
  9.5 1.4 copy-done.4
  11.7 5.7 %collective-permute-start.1 = (bf16[128,16,128]{2,0,1:T(8,128)(2,1)}, bf16[128,16,128]{2,0,1:T(8,128)(2,1)}, u32[]{:S(2)}, u32[]{:S(2)}) collective-permute-start(bf16[128,16,128]{2,0,1:T(8,128)(2,1)} %slice_bitcast_fusion), channel_id=1, source_target_pairs={{0,4},{4,8},{8,12},{12,16},{16,20},{20,24},{24,28},{1,5},{5,9},{9,... | collective-permute-start | bytes 1572872 | tf_op jit(solution)/shard_map/ppermute | solution.py:16
  17.4 1.9 slice_bitcast_fusion.1
  19.3 2.7 collective-permute-start
  26.0 3.5 copy.177
  29.5 1.9 copy.171
  31.4 2.4 convert.3
  33.8 1.5 fusion.73
  35.3 2.0 fusion.65
  38.1 0.9 fusion.171
  39.7 1.9 pad_maximum_fusion
  41.6 1.5 copy-done.1
  43.1 2.1 fusion.44
  45.3 35.2 %all-gather = f32[128,8,128]{2,1,0:T(8,128)} all-gather(f32[16,8,128]{2,1,0:T(8,128)S(1)} %slice_reduce_fusion), channel_id=2, replica_groups=mesh['seq'=8,'batch'=4] {'seq'}, dimensions={0}, use_global_device_ids=true | all-gather | bytes 589824 | tf_op jit(solution)/shard_map/all_gather | solution.py:21
  80.6 30.6 %all-gather.4 = f32[8,16,8]{1,2,0:T(8,128)S(1)} all-gather(f32[1,16,8]{1,2,0:T(8,128)S(1)} %bitcast.246), channel_id=3, replica_groups=mesh['seq'=8,'batch'=4] {'seq'}, dimensions={0}, use_global_device_ids=true | all-gather | bytes 4608 | tf_op jit(solution)/shard_map/all_gather | solution.py:21
  111.2 7.7 %while.34 = (s32[]{:T(128)}, f32[16,8,128]{2,1,0:T(8,128)S(1)}, f32[16,8]{0,1:T(8,128)S(1)}, s32[]{:T(128)}, f32[8,16,8,128]{3,2,1,0:T(8,128)}, /*index=5*/f32[8,16,8]{1,2,0:T(8,128)S(1)}, s32[]{:T(128)}, s32[]{:T(128)}) while((s32[]{:T(128)}, f32[16,8,128]{2,1,0:T(8,128)S(1)}, f32[16,8]{0,1:T(8,128)S(1)}, s32[]{:T(128)}, ...), condition=%wide.region_5.6_spmd.clone, body=%wide.region_4.5_spmd.clone.sunk | while | flops 49540 | bytes 198259 | solution.py:34
  112.1 0.9 add_select_fusion.9
  113.0 0.9 add_select_fusion.9
  113.9 0.9 add_select_fusion.9
  114.8 0.9 add_select_fusion.9
  118.9 3.9 fusion.42
  124.9 6.7 %convolution_bitcast_fusion = f32[4,128,16,128]{3,1,2,0:T(8,128)S(1)} fusion(f32[4,16,8,128]{3,0,2,1:T(4,128)S(1)} %fusion.66, f32[512,16,8]{0,2,1:T(8,128)S(1)} %copy-done.13), kind=kOutput, calls=%fused_computation.42 | convolution fusion | flops 101056512 | bytes 4718592 | tf_op jit(solution)/shard_map/nthr,nhrd->nthd/dot_general | solution.py:155
  131.6 4.5 %copy.193 = f32[4,128,16,128]{3,2,1,0:T(8,128)} copy(f32[4,128,16,128]{3,1,2,0:T(8,128)S(1)} %convolution_bitcast_fusion) | data formatting | bytes 8388608 | tf_op jit(solution)/shard_map/nthr,nhrd->nthd/transpose | solution.py:155
  138.2 1.7 pad_maximum_fusion.2
  139.9 2.9 fusion
  143.5 4.1 fusion.2
  148.4 1.7 fusion.32
  150.7 1.6 copy-done.10
  152.3 6.3 %fusion.27 = f32[4,128,16,128]{3,1,2,0:T(8,128)S(1)} fusion(f32[4,16,256,128]{3,2,1,0:T(8,128)S(1)} %copy-done.10, f32[4,16,128]{2,1,0:T(8,128)S(1)} %get-tuple-element.356, pred[4,16,256]{2,1,0:T(8,128)(4,1)S(1)} %copy-done.26, pred[128,256]{0,1:T(8,128)(4,1)S(1)} %copy-done.21, pred[256]{0:T(512)(128)(4,1)S(1)} %copy-done.42, ...), kind=kOutput, calls=%fused_computation.41 | convolution fusion | flops 555745280 | bytes 16859392 | tf_op jit(solution)/shard_map/nhqk,nkhd->nqhd/dot_general | solution.py:147
  158.6 4.4 %copy.180 = f32[4,128,16,128]{3,2,1,0:T(8,128)} copy(f32[4,128,16,128]{3,1,2,0:T(8,128)S(1)} %fusion.27) | data formatting | bytes 8388608 | tf_op jit(solution)/shard_map/nhqk,nkhd->nqhd/transpose | solution.py:147
  163.1 6.9 %fusion.14 = f32[512,16,128]{2,1,0:T(8,128)S(1)} fusion(f32[4,128,16,128]{3,2,1,0:T(8,128)} %copy.193, f32[4,128,16,128]{3,2,1,0:T(8,128)} %copy.180, f32[512,16]{1,0:T(8,128)S(1)} %copy.182, f32[512,16]{1,0:T(8,128)S(1)} %copy.198), kind=kLoop, calls=%fused_computation.21 | loop fusion | flops 3145728 | bytes 12648448 | tf_op jit(solution)/shard_map/div | solution.py:162
  170.0 14.1 %fusion.23 = f32[512,16]{1,0:T(8,128)S(1)} fusion(f32[512,16,128]{2,1,0:T(8,128)S(1)} %fusion.14, f32[512,16]{1,0:T(8,128)S(1)} %copy.198, bf16[1,512,16,128]{3,2,1,0:T(8,128)(2,1)S(1)} %copy-done.8), kind=kLoop, calls=%fused_computation.33 | loop fusion | flops 4186112 | bytes 6356992 | tf_op jit(solution)/shard_map/reduce_sum | solution.py:164
  185.1 0.9 fusion.122
  186.7 7.5 %fusion.174 = (f32[16,8,128]{2,1,0:T(8,128)S(1)}, f32[4,16,8,128]{3,2,1,0:T(8,128)}) fusion(f32[4,128,16,128]{3,2,1,0:T(8,128)} %convert.3, f32[4,128,16]{1,2,0:T(8,128)S(1)} %get-tuple-element.351, f32[4,128,16]{1,2,0:T(8,128)S(1)} %copy-done.28, f32[512,16,8]{0,2,1:T(8,128)S(1)} %copy-done.14), kind=kOutput, calls=%fused_computation.200 | convolution fusion | flops 103202816 | bytes 4849664 | tf_op jit(solution)/shard_map/nthr,nthd->nhrd/dot_general | solution.py:171
  194.2 31.2 %all-gather.2 = f32[128,8,128]{2,1,0:T(8,128)S(1)} all-gather(f32[16,8,128]{2,1,0:T(8,128)S(1)} %get-tuple-element.358), channel_id=4, replica_groups=mesh['seq'=8,'batch'=4] {'seq'}, dimensions={0}, use_global_device_ids=true | all-gather | bytes 589824 | tf_op jit(solution)/shard_map/all_gather | solution.py:21
  225.4 30.6 %all-gather.5 = f32[8,16,8]{1,2,0:T(8,128)S(1)} all-gather(f32[1,16,8]{1,2,0:T(8,128)S(1)} %bitcast.245), channel_id=5, replica_groups=mesh['seq'=8,'batch'=4] {'seq'}, dimensions={0}, use_global_device_ids=true | all-gather | bytes 4608 | tf_op jit(solution)/shard_map/all_gather | solution.py:21
  257.1 1.6 fusion.106
  258.7 2.6 convolution_add_fusion
  262.2 9.5 %fusion.76 = f32[4,128,16,8]{1,3,2,0:T(8,128)S(1)} fusion(f32[4,128,16,128]{3,2,1,0:T(8,128)} %convert.3, f32[4,128,16]{1,2,0:T(8,128)} %copy-done.31, f32[4,128,16]{1,2,0:T(8,128)} %get-tuple-element.352, f32[4,16,8,128]{3,0,2,1:T(4,128)} %copy-done.15, f32[4,16,8]{2,1,0:T(8,128)} %copy.207, f32[4,128,16]{1,2,0:T(8,128)} %copy-done.30), kind=kOutput, calls=%fused_computation.74 | convolution fusion | flops 102891520 | bytes 4818944 | tf_op jit(solution)/shard_map/nthd,nhrd->nthr/dot_general | solution.py:168
  271.7 2.0 fusion.79
  273.7 4.1 fusion.51
  277.9 4.1 fusion.57
  282.1 3.1 fusion.47
  285.1 7.2 %fusion.18 = bf16[1,512,16,128]{3,2,1,0:T(8,128)(2,1)} fusion(f32[512,16]{1,0:T(8,128)S(1)} %copy.198, f32[512,16]{1,0:T(8,128)S(1)} %copy.182, f32[1,512,16,128]{3,2,1,0:T(8,128)} %bitcast.221, f32[1,512,16,128]{3,2,1,0:T(8,128)} %bitcast.222), kind=kLoop, calls=%fused_computation.27 | loop fusion | flops 4194304 | bytes 10551296 | tf_op jit(solution)/shard_map/convert_element_type | solution.py:203
  292.4 117.7 %all-reduce.4.cloned.1.call-done = (f32[16,128,8]{1,2,0:T(8,128)}, f32[16,128,8]{1,2,0:T(8,128)}) async-done(((f32[16,128,8]{1,2,0:T(8,128)}, f32[16,128,8]{1,2,0:T(8,128)}), (f32[16,128,8]{1,2,0:T(8,128)}, f32[16,128,8]{1,2,0:T(8,128)})) %all-reduce.4.cloned.1.call-update) | async-done | bytes 131088 | tf_op jit(solution)/shard_map/psum | solution.py:202
  410.1 1.5 copy.353
  411.5 1.5 copy.354
  (170 shorter events, 19.9 us)
Async XLA Ops:
  7.2 26.6 %copy-start = (bf16[1,512,16,128]{3,2,1,0:T(8,128)(2,1)S(1)}, bf16[1,512,16,128]{3,2,1,0:T(8,128)(2,1)}, u32[]{:S(2)}) copy-start(bf16[1,512,16,128]{3,2,1,0:T(8,128)(2,1)} %param.11) | copy-start | bytes 6291460
  7.2 16.6 %copy-start.37 = (s32[1,16,32]{2,1,0:T(8,128)S(1)}, s32[1,16,32]{2,1,0:T(8,128)}, u32[]{:S(2)}) copy-start(s32[1,16,32]{2,1,0:T(8,128)} %param.14) | copy-start | bytes 6148
  7.2 402.9 %all-reduce.4.cloned.1.call-start = ((), (), s32[]{:S(2)}) async-start(), calls=%async_computation | async-start | bytes 262144 | tf_op jit(solution)/shard_map/psum | solution.py:202
  9.5 1.4 copy-start.4
  11.7 23.6 %collective-permute-start.1 = (bf16[128,16,128]{2,0,1:T(8,128)(2,1)}, bf16[128,16,128]{2,0,1:T(8,128)(2,1)}, u32[]{:S(2)}, u32[]{:S(2)}) collective-permute-start(bf16[128,16,128]{2,0,1:T(8,128)(2,1)} %slice_bitcast_fusion), channel_id=1, source_target_pairs={{0,4},{4,8},{8,12},{12,16},{16,20},{20,24},{24,28},{1,5},{5,9},{9,... | collective-permute-start | bytes 1572872 | tf_op jit(solution)/shard_map/ppermute | solution.py:16
  19.3 20.4 %collective-permute-start = (bf16[128,16,128]{2,1,0:T(8,128)(2,1)}, bf16[128,16,128]{2,1,0:T(8,128)(2,1)S(1)}, u32[]{:S(2)}, u32[]{:S(2)}) collective-permute-start(bf16[128,16,128]{2,1,0:T(8,128)(2,1)} %slice_bitcast_fusion.1), channel_id=1, source_target_pairs={{0,4},{4,8},{8,12},{12,16},{16,20},{20,24},{24,28},{1,5},{5,9},{9,... | collective-permute-start | bytes 1572872 | tf_op jit(solution)/shard_map/ppermute | solution.py:16
  22.0 15.3 %copy-start.32 = (f32[640]{0:T(1024)}, f32[640]{0:T(1024)S(1)}, u32[]{:S(2)}) copy-start(f32[640]{0:T(1024)S(1)} %fusion.149) | copy-start | bytes 7684
  22.0 114.2 %copy-start.34 = (s32[4]{0:T(128)}, s32[4]{0:T(128)S(1)}, u32[]{:S(2)}) copy-start(s32[4]{0:T(128)S(1)} %iota_add_fusion.1) | copy-start | bytes 52
  25.4 4.1 copy-start.3
  29.5 1.9 copy-start.7
  31.4 2.4 copy-start.27
  31.4 4.0 copy-start.5
  31.4 4.0 copy-start.44
  33.8 3.5 copy-start.19
  37.3 0.7 copy-start.17
  39.7 3.4 copy-start.12
  41.6 1.5 copy-start.1
  111.2 12.2 %copy-start.38 = (f32[5]{0:T(128)S(1)}, f32[5]{0:T(128)}, u32[]{:S(2)}) copy-start(f32[5]{0:T(128)} %broadcast_subtract_fusion) | copy-start | bytes 64
  111.2 12.2 %copy-start.40 = (f32[5]{0:T(128)S(1)}, f32[5]{0:T(128)}, u32[]{:S(2)}) copy-start(f32[5]{0:T(128)} %compare_convert_fusion.1) | copy-start | bytes 64
  118.9 6.0 %copy-start.13 = (f32[512,16,8]{0,2,1:T(8,128)S(1)}, f32[512,16,8]{0,2,1:T(8,128)}, u32[]{:S(2)}) copy-start(f32[512,16,8]{0,2,1:T(8,128)} %fusion.73) | copy-start | bytes 786436
  124.2 0.7 copy-start.15
  131.6 4.7 %copy-start.29 = (f32[5,16,8]{1,0,2:T(8,128)S(1)}, f32[5,16,8]{1,0,2:T(8,128)}, u32[]{:S(2)}) copy-start(f32[5,16,8]{1,0,2:T(8,128)} %copy.195) | copy-start | bytes 7684
  131.6 5.8 %copy-start.14 = (f32[512,16,8]{0,2,1:T(8,128)S(1)}, f32[512,16,8]{0,2,1:T(8,128)}, u32[]{:S(2)}) copy-start(f32[512,16,8]{0,2,1:T(8,128)} %fusion.73) | copy-start | bytes 786436
  137.5 2.4 copy-start.11
  137.5 2.4 copy-start.21
  137.5 2.4 copy-start.26
  137.5 2.4 copy-start.42
  138.2 10.1 %copy-start.23 = (f32[4,16,1,128]{3,2,1,0:T(1,128)}, f32[4,16,1,128]{3,2,1,0:T(1,128)S(1)}, u32[]{:S(2)}) copy-start(f32[4,16,1,128]{3,2,1,0:T(1,128)S(1)} %fusion.112) | copy-start | bytes 98308
  142.8 4.8 %copy-start.9 = (f32[4,16,256,128]{3,2,1,0:T(8,128)}, f32[4,16,256,128]{3,2,1,0:T(8,128)S(1)}, u32[]{:S(2)}) copy-start(f32[4,16,256,128]{3,2,1,0:T(8,128)S(1)} %get-tuple-element.357) | copy-start | bytes 25165828
  148.4 3.9 copy-start.10
  158.6 4.4 %copy-start.22 = (f32[4,2,8,128]{3,2,0,1:T(8,128)S(1)}, f32[4,2,8,128]{3,2,0,1:T(8,128)}, u32[]{:S(2)}) copy-start(f32[4,2,8,128]{3,2,0,1:T(8,128)} %copy.331) | copy-start | bytes 98308
  163.1 6.9 %copy-start.8 = (bf16[1,512,16,128]{3,2,1,0:T(8,128)(2,1)S(1)}, bf16[1,512,16,128]{3,2,1,0:T(8,128)(2,1)}, u32[]{:S(2)}) copy-start(bf16[1,512,16,128]{3,2,1,0:T(8,128)(2,1)} %param.17) | copy-start | bytes 6291460
  170.0 14.2 %copy-start.24 = (f32[4,16,1,128]{3,2,1,0:T(1,128)S(1)}, f32[4,16,1,128]{3,2,1,0:T(1,128)}, u32[]{:S(2)}) copy-start(f32[4,16,1,128]{3,2,1,0:T(1,128)} %copy-done.23) | copy-start | bytes 98308
  170.0 15.0 %copy-start.35 = (s32[4]{0:T(128)S(1)}, s32[4]{0:T(128)}, u32[]{:S(2)}) copy-start(s32[4]{0:T(128)} %copy-done.34) | copy-start | bytes 52
  170.0 16.6 %copy-start.28 = (f32[4,128,16]{1,2,0:T(8,128)S(1)}, f32[4,128,16]{1,2,0:T(8,128)}, u32[]{:S(2)}) copy-start(f32[4,128,16]{1,2,0:T(8,128)} %get-tuple-element.352) | copy-start | bytes 98308
  184.3 9.9 %copy-start.30 = (f32[4,128,16]{1,2,0:T(8,128)}, f32[4,128,16]{1,2,0:T(8,128)S(1)}, u32[]{:S(2)}) copy-start(f32[4,128,16]{1,2,0:T(8,128)S(1)} %get-tuple-element.350) | copy-start | bytes 98308
  184.3 9.9 %copy-start.31 = (f32[4,128,16]{1,2,0:T(8,128)}, f32[4,128,16]{1,2,0:T(8,128)S(1)}, u32[]{:S(2)}) copy-start(f32[4,128,16]{1,2,0:T(8,128)S(1)} %get-tuple-element.351) | copy-start | bytes 98308
  186.6 69.3 %copy-start.25 = (f32[16,8]{0,1:T(8,128)S(1)}, f32[16,8]{0,1:T(8,128)}, u32[]{:S(2)}) copy-start(f32[16,8]{0,1:T(8,128)} %custom-call.3) | copy-start | bytes 1540
  186.6 70.1 %copy-start.36 = (s32[4]{0:T(128)S(1)}, s32[4]{0:T(128)}, u32[]{:S(2)}) copy-start(s32[4]{0:T(128)} %copy-done.34) | copy-start | bytes 52
  186.6 70.1 %copy-start.39 = (f32[5]{0:T(128)S(1)}, f32[5]{0:T(128)}, u32[]{:S(2)}) copy-start(f32[5]{0:T(128)} %broadcast_subtract_fusion) | copy-start | bytes 64
  186.6 70.1 %copy-start.41 = (f32[5]{0:T(128)S(1)}, f32[5]{0:T(128)}, u32[]{:S(2)}) copy-start(f32[5]{0:T(128)} %compare_convert_fusion.1) | copy-start | bytes 64
  186.6 70.1 %copy-start.43 = (f32[5]{0:T(128)S(1)}, f32[5]{0:T(128)}, u32[]{:S(2)}) copy-start(f32[5]{0:T(128)} %compare_convert_fusion) | copy-start | bytes 64
  271.7 2.0 copy-start.2
  271.7 2.0 copy-start.16
  277.8 4.2 copy-start.6
  277.8 4.2 copy-start.18
  277.8 4.2 copy-start.20
  277.9 4.2 %copy-start.33 = (f32[640]{0:T(1024)S(1)}, f32[640]{0:T(1024)}, u32[]{:S(2)}) copy-start(f32[640]{0:T(1024)} %copy-done.32) | copy-start | bytes 7684
Sparse Core Ops, SparseCore 0:
  285.3 124.7 all-reduce.3
where the time goes:
time: 427 us; the launch traced here: 420 us
  blocking collectives  128 us (30%)
  waiting for transfers between devices  118 us (28%)
  matrix products  64.9 us (15%)
  other arithmetic  52 us (12%)
  local copies, waits for them, and re-layouts  33.3 us (8%)
  between operations  15.1 us (4%)
  starting transfers between devices  8.39 us (2%)
    all_gather x4, blocking collectives, prefix(): everything = jax.tree.map(lambda part: lax.all_gather(part, axis), shard)  128 us
    psum x1, waiting for transfers between devices, body(): grad_q, grad_k = lax.psum((grad_q, grad_k), ('seq', 'batch'))  118 us
    reduce_sum x1, other arithmetic, body(): ratio_grad = -jnp.sum(delta * out, -1)  14.1 us
    unnamed x93, local copies, waits for them, and re-layouts  11.3 us
    dot_general x1, matrix products, body(): jnp.einsum('nthd,nhrd->nthr', grad_num, state, precision=HIGHEST)  9.54 us
  transfers between devices with their start and end apart: 3, of which 1 were waited for; matrix products, arithmetic and copies ran while one was open for 6% of the time, Pallas kernels for 0%

commit v1 on v0

--- a/solution.py
+++ b/solution.py
@@ -8,6 +8,11 @@
 WINDOW = 256
 HIGHEST = lax.Precision.HIGHEST
 feature_shift = 1.5
+
+
+def manage_the_state(xs):
+    taken_in = lax.psum(xs, axis_name="seq")
+    return lax.psum(taken_in, axis_name="batch")
 
 
 def passed_along(value, axis, steps):
@@ -199,7 +204,7 @@
     grad_pre_q = grad_fq.reshape(tokens, heads, rank) * jax.nn.sigmoid(pre_q)
     grad_q = jnp.einsum("thd,thr->hdr", q_rows.astype(jnp.float32), grad_pre_q, precision=HIGHEST)
     grad_k = jnp.einsum("thd,thr->hdr", ext_keys.astype(jnp.float32), grad_pre_k, precision=HIGHEST)
-    grad_q, grad_k = lax.psum((grad_q, grad_k), ("seq", "batch"))
+    grad_q, grad_k = manage_the_state((grad_q, grad_k))
     return (out.astype(jnp.bfloat16)[None], grad_q, grad_k)
 
 

time: 427 us -> 406 us (0.951)
  waiting for transfers between devices: 118 us -> 96.8 us
    psum x1 -> x2, waiting for transfers between devices: 118 us -> 96.8 us  [the longest x1 70.7 us: manage_the_state(): taken_in = lax.psum(xs, axis_name='seq')]
  transfers between devices with their start and end apart: 3 -> 4, of which waited for: 1 -> 2; matrix products, arithmetic and copies ran while one was open for 6% -> 6% of each run, Pallas kernels for 0% -> 0%
where the time goes in v1:
time: 406 us; the launch traced here: 399 us
  blocking collectives  128 us (32%)
  waiting for transfers between devices  96.8 us (24%)
  matrix products  64.9 us (16%)
  other arithmetic  51.9 us (13%)
  local copies, waits for them, and re-layouts  33.3 us (8%)
  between operations  15.1 us (4%)
  starting transfers between devices  8.43 us (2%)
    all_gather x4, blocking collectives, prefix(): everything = jax.tree.map(lambda part: lax.all_gather(part, axis), shard)  128 us
    psum x1, waiting for transfers between devices, manage_the_state(): taken_in = lax.psum(xs, axis_name='seq')  70.7 us
    psum x1, waiting for transfers between devices, manage_the_state(): return lax.psum(taken_in, axis_name='batch')  26.1 us
    reduce_sum x1, other arithmetic, body(): ratio_grad = -jnp.sum(delta * out, -1)  14.1 us
    unnamed x93, local copies, waits for them, and re-layouts  11.3 us
    dot_general x1, matrix products, body(): jnp.einsum('nthd,nhrd->nthr', grad_num, state, precision=HIGHEST)  9.54 us
    ppermute x2, starting transfers between devices, passed_along(): lax.ppermute(value, axis, [(source, source + steps) for source in range(f...  8.35 us
  transfers between devices with their start and end apart: 4, of which 2 were waited for; matrix products, arithmetic and copies ran while one was open for 6% of the time, Pallas kernels for 0%

profile of v1, /device:TPU:0, one launch (start us, length us, event | category | flops | bytes accessed | tf_op | source)
XLA Modules:
  0.0 399.4 jit_solution(13520086422673321246)
XLA Ops:
  7.2 2.3 copy.332
  9.5 1.4 copy-done.4
  11.7 5.7 %collective-permute-start.1 = (bf16[128,16,128]{2,0,1:T(8,128)(2,1)}, bf16[128,16,128]{2,0,1:T(8,128)(2,1)}, u32[]{:S(2)}, u32[]{:S(2)}) collective-permute-start(bf16[128,16,128]{2,0,1:T(8,128)(2,1)} %slice_bitcast_fusion), channel_id=1, source_target_pairs={{0,4},{4,8},{8,12},{12,16},{16,20},{20,24},{24,28},{1,5},{5,9},{9,... | collective-permute-start | bytes 1572872 | tf_op jit(solution)/shard_map/ppermute | solution.py:21
  17.4 1.9 slice_bitcast_fusion.1
  19.3 2.7 collective-permute-start
  25.8 3.5 copy.177
  29.3 1.9 copy.171
  31.3 2.4 convert.3
  33.7 1.5 fusion.73
  35.2 2.0 fusion.65
  37.9 0.9 fusion.171
  39.6 1.9 pad_maximum_fusion
  41.5 1.5 copy-done.1
  43.0 2.1 fusion.44
  45.1 35.4 %all-gather = f32[128,8,128]{2,1,0:T(8,128)} all-gather(f32[16,8,128]{2,1,0:T(8,128)S(1)} %slice_reduce_fusion), channel_id=2, replica_groups=mesh['seq'=8,'batch'=4] {'seq'}, dimensions={0}, use_global_device_ids=true | all-gather | bytes 589824 | tf_op jit(solution)/shard_map/all_gather | solution.py:26
  80.6 30.6 %all-gather.4 = f32[8,16,8]{1,2,0:T(8,128)S(1)} all-gather(f32[1,16,8]{1,2,0:T(8,128)S(1)} %bitcast.246), channel_id=3, replica_groups=mesh['seq'=8,'batch'=4] {'seq'}, dimensions={0}, use_global_device_ids=true | all-gather | bytes 4608 | tf_op jit(solution)/shard_map/all_gather | solution.py:26
  111.2 7.7 %while.34 = (s32[]{:T(128)}, f32[16,8,128]{2,1,0:T(8,128)S(1)}, f32[16,8]{0,1:T(8,128)S(1)}, s32[]{:T(128)}, f32[8,16,8,128]{3,2,1,0:T(8,128)}, /*index=5*/f32[8,16,8]{1,2,0:T(8,128)S(1)}, s32[]{:T(128)}, s32[]{:T(128)}) while((s32[]{:T(128)}, f32[16,8,128]{2,1,0:T(8,128)S(1)}, f32[16,8]{0,1:T(8,128)S(1)}, s32[]{:T(128)}, ...), condition=%wide.region_5.6_spmd.clone, body=%wide.region_4.5_spmd.clone.sunk | while | flops 49540 | bytes 198259 | solution.py:39
  114.8 0.9 add_select_fusion.9
  115.7 0.9 add_select_fusion.9
  118.9 3.9 fusion.42
  124.9 6.7 %convolution_bitcast_fusion = f32[4,128,16,128]{3,1,2,0:T(8,128)S(1)} fusion(f32[4,16,8,128]{3,0,2,1:T(4,128)S(1)} %fusion.66, f32[512,16,8]{0,2,1:T(8,128)S(1)} %copy-done.13), kind=kOutput, calls=%fused_computation.42 | convolution fusion | flops 101056512 | bytes 4718592 | tf_op jit(solution)/shard_map/nthr,nhrd->nthd/dot_general | solution.py:160
  131.6 4.5 %copy.193 = f32[4,128,16,128]{3,2,1,0:T(8,128)} copy(f32[4,128,16,128]{3,1,2,0:T(8,128)S(1)} %convolution_bitcast_fusion) | data formatting | bytes 8388608 | tf_op jit(solution)/shard_map/nthr,nhrd->nthd/transpose | solution.py:160
  136.5 0.9 convolution_add_fusion.3
  138.2 1.7 pad_maximum_fusion.2
  139.9 2.9 fusion
  143.5 4.1 %fusion.2 = f32[4,16,128]{2,1,0:T(8,128)S(1)} fusion(f32[4,16,256,128]{3,2,1,0:T(8,128)S(1)} %get-tuple-element.359, f32[4,16,128]{2,1,0:T(8,128)S(1)} %get-tuple-element.358, pred[4,16,256]{2,1,0:T(8,128)(4,1)S(1)} %copy-done.26, pred[128,256]{0,1:T(8,128)(4,1)S(1)} %copy-done.21, pred[256]{0:T(512)(128)(4,1)S(1)} %copy-done.42), kind=kLoop, calls=%fused_computation.9 | loop fusion | flops 10477568 | bytes 8503552 | tf_op jit(solution)/shard_map/reduce_sum | solution.py:151
  148.4 1.7 fusion.32
  150.7 1.6 copy-done.10
  152.3 6.3 %fusion.27 = f32[4,128,16,128]{3,1,2,0:T(8,128)S(1)} fusion(f32[4,16,256,128]{3,2,1,0:T(8,128)S(1)} %copy-done.10, f32[4,16,128]{2,1,0:T(8,128)S(1)} %get-tuple-element.358, pred[4,16,256]{2,1,0:T(8,128)(4,1)S(1)} %copy-done.26, pred[128,256]{0,1:T(8,128)(4,1)S(1)} %copy-done.21, pred[256]{0:T(512)(128)(4,1)S(1)} %copy-done.42, ...), kind=kOutput, calls=%fused_computation.41 | convolution fusion | flops 555745280 | bytes 16859392 | tf_op jit(solution)/shard_map/nhqk,nkhd->nqhd/dot_general | solution.py:152
  158.6 4.4 %copy.180 = f32[4,128,16,128]{3,2,1,0:T(8,128)} copy(f32[4,128,16,128]{3,1,2,0:T(8,128)S(1)} %fusion.27) | data formatting | bytes 8388608 | tf_op jit(solution)/shard_map/nhqk,nkhd->nqhd/transpose | solution.py:152
  163.1 6.9 %fusion.14 = f32[512,16,128]{2,1,0:T(8,128)S(1)} fusion(f32[4,128,16,128]{3,2,1,0:T(8,128)} %copy.193, f32[4,128,16,128]{3,2,1,0:T(8,128)} %copy.180, f32[512,16]{1,0:T(8,128)S(1)} %copy.182, f32[512,16]{1,0:T(8,128)S(1)} %copy.198), kind=kLoop, calls=%fused_computation.21 | loop fusion | flops 3145728 | bytes 12648448 | tf_op jit(solution)/shard_map/div | solution.py:167
  170.0 14.1 %fusion.23 = f32[512,16]{1,0:T(8,128)S(1)} fusion(f32[512,16,128]{2,1,0:T(8,128)S(1)} %fusion.14, f32[512,16]{1,0:T(8,128)S(1)} %copy.198, bf16[1,512,16,128]{3,2,1,0:T(8,128)(2,1)S(1)} %copy-done.8), kind=kLoop, calls=%fused_computation.33 | loop fusion | flops 4186112 | bytes 6356992 | tf_op jit(solution)/shard_map/reduce_sum | solution.py:169
  185.1 0.9 fusion.122
  186.7 7.5 %fusion.174 = (f32[16,8,128]{2,1,0:T(8,128)S(1)}, f32[4,16,8,128]{3,2,1,0:T(8,128)}) fusion(f32[4,128,16,128]{3,2,1,0:T(8,128)} %convert.3, f32[4,128,16]{1,2,0:T(8,128)S(1)} %get-tuple-element.353, f32[4,128,16]{1,2,0:T(8,128)S(1)} %copy-done.28, f32[512,16,8]{0,2,1:T(8,128)S(1)} %copy-done.14), kind=kOutput, calls=%fused_computation.200 | convolution fusion | flops 103202816 | bytes 4849664 | tf_op jit(solution)/shard_map/nthr,nthd->nhrd/dot_general | solution.py:176
  194.2 31.2 %all-gather.2 = f32[128,8,128]{2,1,0:T(8,128)S(1)} all-gather(f32[16,8,128]{2,1,0:T(8,128)S(1)} %get-tuple-element.360), channel_id=4, replica_groups=mesh['seq'=8,'batch'=4] {'seq'}, dimensions={0}, use_global_device_ids=true | all-gather | bytes 589824 | tf_op jit(solution)/shard_map/all_gather | solution.py:26
  225.4 30.6 %all-gather.5 = f32[8,16,8]{1,2,0:T(8,128)S(1)} all-gather(f32[1,16,8]{1,2,0:T(8,128)S(1)} %bitcast.245), channel_id=5, replica_groups=mesh['seq'=8,'batch'=4] {'seq'}, dimensions={0}, use_global_device_ids=true | all-gather | bytes 4608 | tf_op jit(solution)/shard_map/all_gather | solution.py:26
  257.2 1.6 fusion.106
  258.7 2.6 convolution_add_fusion
  262.2 9.5 %fusion.76 = f32[4,128,16,8]{1,3,2,0:T(8,128)S(1)} fusion(f32[4,128,16,128]{3,2,1,0:T(8,128)} %convert.3, f32[4,128,16]{1,2,0:T(8,128)} %copy-done.31, f32[4,128,16]{1,2,0:T(8,128)} %get-tuple-element.354, f32[4,16,8,128]{3,0,2,1:T(4,128)} %copy-done.15, f32[4,16,8]{2,1,0:T(8,128)} %copy.207, f32[4,128,16]{1,2,0:T(8,128)} %copy-done.30), kind=kOutput, calls=%fused_computation.74 | convolution fusion | flops 102891520 | bytes 4818944 | tf_op jit(solution)/shard_map/nthd,nhrd->nthr/dot_general | solution.py:173
  271.7 2.0 fusion.79
  273.7 4.1 %fusion.51 = f32[5,128,16,8]{1,3,2,0:T(8,128)S(1)} fusion(bf16[5,128,16,128]{3,2,1,0:T(8,128)(2,1)S(1)} %bitcast.225, f32[5,16,8,128]{3,0,2,1:T(8,128)S(1)} %copy-done.16, f32[5,16,8]{2,1,0:T(8,128)S(1)} %copy.214), kind=kOutput, calls=%fused_computation.62 | convolution fusion | flops 125911040 | bytes 3279360 | tf_op jit(solution)/shard_map/nhrd,nthd->nthr/dot_general | solution.py:198
  277.9 4.1 %fusion.57 = f32[5,128,16,8]{1,3,2,0:T(8,128)S(1)} fusion(bf16[5,128,16,128]{3,2,1,0:T(8,128)(2,1)S(1)} %bitcast.226, f32[5,16,8,128]{3,0,2,1:T(8,128)S(1)} %fusion.106, f32[5,16,8]{2,1,0:T(8,128)S(1)} %copy.219), kind=kOutput, calls=%fused_computation.64 | convolution fusion | flops 125911040 | bytes 3279360 | tf_op jit(solution)/shard_map/nhrd,nthd->nthr/dot_general | solution.py:199
  282.1 3.1 fusion.47
  285.2 70.7 %all-reduce.6.cloned.1.call-done = (f32[16,128,8]{1,2,0:T(8,128)}, f32[16,128,8]{1,2,0:T(8,128)}) async-done(((f32[16,128,8]{1,2,0:T(8,128)}, f32[16,128,8]{1,2,0:T(8,128)}), (f32[16,128,8]{1,2,0:T(8,128)}, f32[16,128,8]{1,2,0:T(8,128)})) %all-reduce.6.cloned.1.call-update) | async-done | bytes 131088 | tf_op jit(solution)/shard_map/psum | solution.py:14
  355.9 7.2 %fusion.18 = bf16[1,512,16,128]{3,2,1,0:T(8,128)(2,1)} fusion(f32[512,16]{1,0:T(8,128)S(1)} %copy.198, f32[512,16]{1,0:T(8,128)S(1)} %copy.182, f32[1,512,16,128]{3,2,1,0:T(8,128)} %bitcast.221, f32[1,512,16,128]{3,2,1,0:T(8,128)} %bitcast.222), kind=kLoop, calls=%fused_computation.27 | loop fusion | flops 4194304 | bytes 10551296 | tf_op jit(solution)/shard_map/convert_element_type | solution.py:208
  363.2 26.1 %all-reduce.8.cloned.1.call-done = (f32[16,128,8]{1,2,0:T(8,128)}, f32[16,128,8]{1,2,0:T(8,128)}) async-done(((f32[16,128,8]{1,2,0:T(8,128)}, f32[16,128,8]{1,2,0:T(8,128)}), (f32[16,128,8]{1,2,0:T(8,128)}, f32[16,128,8]{1,2,0:T(8,128)})) %all-reduce.8.cloned.1.call-update) | async-done | bytes 131088 | tf_op jit(solution)/shard_map/psum | solution.py:15
  389.3 1.5 copy.355
  390.7 1.5 copy.356
  (173 shorter events, 20.7 us)
Async XLA Ops:
  7.2 26.5 %copy-start = (bf16[1,512,16,128]{3,2,1,0:T(8,128)(2,1)S(1)}, bf16[1,512,16,128]{3,2,1,0:T(8,128)(2,1)}, u32[]{:S(2)}) copy-start(bf16[1,512,16,128]{3,2,1,0:T(8,128)(2,1)} %param.11) | copy-start | bytes 6291460
  7.2 16.6 %copy-start.37 = (s32[1,16,32]{2,1,0:T(8,128)S(1)}, s32[1,16,32]{2,1,0:T(8,128)}, u32[]{:S(2)}) copy-start(s32[1,16,32]{2,1,0:T(8,128)} %param.14) | copy-start | bytes 6148
  7.2 348.7 %all-reduce.6.cloned.1.call-start = ((), (), s32[]{:S(2)}) async-start(), calls=%async_computation | async-start | bytes 262144 | tf_op jit(solution)/shard_map/psum | solution.py:14
  9.5 1.4 copy-start.4
  11.7 23.5 %collective-permute-start.1 = (bf16[128,16,128]{2,0,1:T(8,128)(2,1)}, bf16[128,16,128]{2,0,1:T(8,128)(2,1)}, u32[]{:S(2)}, u32[]{:S(2)}) collective-permute-start(bf16[128,16,128]{2,0,1:T(8,128)(2,1)} %slice_bitcast_fusion), channel_id=1, source_target_pairs={{0,4},{4,8},{8,12},{12,16},{16,20},{20,24},{24,28},{1,5},{5,9},{9,... | collective-permute-start | bytes 1572872 | tf_op jit(solution)/shard_map/ppermute | solution.py:21
  19.3 20.3 %collective-permute-start = (bf16[128,16,128]{2,1,0:T(8,128)(2,1)}, bf16[128,16,128]{2,1,0:T(8,128)(2,1)S(1)}, u32[]{:S(2)}, u32[]{:S(2)}) collective-permute-start(bf16[128,16,128]{2,1,0:T(8,128)(2,1)} %slice_bitcast_fusion.1), channel_id=1, source_target_pairs={{0,4},{4,8},{8,12},{12,16},{16,20},{20,24},{24,28},{1,5},{5,9},{9,... | collective-permute-start | bytes 1572872 | tf_op jit(solution)/shard_map/ppermute | solution.py:21
  22.0 15.2 %copy-start.32 = (f32[640]{0:T(1024)}, f32[640]{0:T(1024)S(1)}, u32[]{:S(2)}) copy-start(f32[640]{0:T(1024)S(1)} %fusion.149) | copy-start | bytes 7684
  22.0 114.2 %copy-start.34 = (s32[4]{0:T(128)}, s32[4]{0:T(128)S(1)}, u32[]{:S(2)}) copy-start(s32[4]{0:T(128)S(1)} %iota_add_fusion.1) | copy-start | bytes 52
  25.2 4.1 %copy-start.3 = (bf16[1,512,16,128]{3,2,1,0:T(8,128)(2,1)S(1)}, bf16[1,512,16,128]{3,2,1,0:T(8,128)(2,1)}, u32[]{:S(2)}) copy-start(bf16[1,512,16,128]{3,2,1,0:T(8,128)(2,1)} %param.13) | copy-start | bytes 6291460
  29.3 1.9 copy-start.7
  31.2 2.4 copy-start.27
  31.2 3.9 copy-start.5
  31.2 3.9 copy-start.44
  33.6 3.5 copy-start.19
  39.6 3.4 copy-start.12
  41.5 1.5 copy-start.1
  111.2 12.2 %copy-start.38 = (f32[5]{0:T(128)S(1)}, f32[5]{0:T(128)}, u32[]{:S(2)}) copy-start(f32[5]{0:T(128)} %broadcast_subtract_fusion) | copy-start | bytes 64
  111.2 12.2 %copy-start.40 = (f32[5]{0:T(128)S(1)}, f32[5]{0:T(128)}, u32[]{:S(2)}) copy-start(f32[5]{0:T(128)} %compare_convert_fusion.1) | copy-start | bytes 64
  118.8 6.0 %copy-start.13 = (f32[512,16,8]{0,2,1:T(8,128)S(1)}, f32[512,16,8]{0,2,1:T(8,128)}, u32[]{:S(2)}) copy-start(f32[512,16,8]{0,2,1:T(8,128)} %fusion.73) | copy-start | bytes 786436
  124.1 0.8 copy-start.15
  131.6 4.7 %copy-start.29 = (f32[5,16,8]{1,0,2:T(8,128)S(1)}, f32[5,16,8]{1,0,2:T(8,128)}, u32[]{:S(2)}) copy-start(f32[5,16,8]{1,0,2:T(8,128)} %copy.195) | copy-start | bytes 7684
  131.6 5.9 %copy-start.14 = (f32[512,16,8]{0,2,1:T(8,128)S(1)}, f32[512,16,8]{0,2,1:T(8,128)}, u32[]{:S(2)}) copy-start(f32[512,16,8]{0,2,1:T(8,128)} %fusion.73) | copy-start | bytes 786436
  137.5 2.4 copy-start.11
  137.5 2.4 copy-start.21
  137.5 2.4 copy-start.26
  137.5 2.4 copy-start.42
  138.2 10.1 %copy-start.23 = (f32[4,16,1,128]{3,2,1,0:T(1,128)}, f32[4,16,1,128]{3,2,1,0:T(1,128)S(1)}, u32[]{:S(2)}) copy-start(f32[4,16,1,128]{3,2,1,0:T(1,128)S(1)} %fusion.112) | copy-start | bytes 98308
  142.8 4.8 %copy-start.9 = (f32[4,16,256,128]{3,2,1,0:T(8,128)}, f32[4,16,256,128]{3,2,1,0:T(8,128)S(1)}, u32[]{:S(2)}) copy-start(f32[4,16,256,128]{3,2,1,0:T(8,128)S(1)} %get-tuple-element.359) | copy-start | bytes 25165828
  148.4 3.9 copy-start.10
  158.6 4.4 %copy-start.22 = (f32[4,2,8,128]{3,2,0,1:T(8,128)S(1)}, f32[4,2,8,128]{3,2,0,1:T(8,128)}, u32[]{:S(2)}) copy-start(f32[4,2,8,128]{3,2,0,1:T(8,128)} %copy.331) | copy-start | bytes 98308
  163.1 6.9 %copy-start.8 = (bf16[1,512,16,128]{3,2,1,0:T(8,128)(2,1)S(1)}, bf16[1,512,16,128]{3,2,1,0:T(8,128)(2,1)}, u32[]{:S(2)}) copy-start(bf16[1,512,16,128]{3,2,1,0:T(8,128)(2,1)} %param.17) | copy-start | bytes 6291460
  170.0 14.2 %copy-start.24 = (f32[4,16,1,128]{3,2,1,0:T(1,128)S(1)}, f32[4,16,1,128]{3,2,1,0:T(1,128)}, u32[]{:S(2)}) copy-start(f32[4,16,1,128]{3,2,1,0:T(1,128)} %copy-done.23) | copy-start | bytes 98308
  170.0 15.0 %copy-start.35 = (s32[4]{0:T(128)S(1)}, s32[4]{0:T(128)}, u32[]{:S(2)}) copy-start(s32[4]{0:T(128)} %copy-done.34) | copy-start | bytes 52
  170.0 16.6 %copy-start.28 = (f32[4,128,16]{1,2,0:T(8,128)S(1)}, f32[4,128,16]{1,2,0:T(8,128)}, u32[]{:S(2)}) copy-start(f32[4,128,16]{1,2,0:T(8,128)} %get-tuple-element.354) | copy-start | bytes 98308
  184.2 9.9 %copy-start.30 = (f32[4,128,16]{1,2,0:T(8,128)}, f32[4,128,16]{1,2,0:T(8,128)S(1)}, u32[]{:S(2)}) copy-start(f32[4,128,16]{1,2,0:T(8,128)S(1)} %get-tuple-element.352) | copy-start | bytes 98308
  184.3 9.9 %copy-start.31 = (f32[4,128,16]{1,2,0:T(8,128)}, f32[4,128,16]{1,2,0:T(8,128)S(1)}, u32[]{:S(2)}) copy-start(f32[4,128,16]{1,2,0:T(8,128)S(1)} %get-tuple-element.353) | copy-start | bytes 98308
  186.6 69.3 %copy-start.25 = (f32[16,8]{0,1:T(8,128)S(1)}, f32[16,8]{0,1:T(8,128)}, u32[]{:S(2)}) copy-start(f32[16,8]{0,1:T(8,128)} %custom-call.3) | copy-start | bytes 1540
  186.6 70.1 %copy-start.36 = (s32[4]{0:T(128)S(1)}, s32[4]{0:T(128)}, u32[]{:S(2)}) copy-start(s32[4]{0:T(128)} %copy-done.34) | copy-start | bytes 52
  186.6 70.1 %copy-start.39 = (f32[5]{0:T(128)S(1)}, f32[5]{0:T(128)}, u32[]{:S(2)}) copy-start(f32[5]{0:T(128)} %broadcast_subtract_fusion) | copy-start | bytes 64
  186.6 70.1 %copy-start.41 = (f32[5]{0:T(128)S(1)}, f32[5]{0:T(128)}, u32[]{:S(2)}) copy-start(f32[5]{0:T(128)} %compare_convert_fusion.1) | copy-start | bytes 64
  186.6 70.1 %copy-start.43 = (f32[5]{0:T(128)S(1)}, f32[5]{0:T(128)}, u32[]{:S(2)}) copy-start(f32[5]{0:T(128)} %compare_convert_fusion) | copy-start | bytes 64
  271.7 2.0 copy-start.2
  271.7 2.0 copy-start.16
  277.9 4.2 %copy-start.6 = (bf16[1,512,16,128]{3,1,2,0:T(8,128)(2,1)S(1)}, bf16[1,512,16,128]{3,1,2,0:T(8,128)(2,1)}, u32[]{:S(2)}) copy-start(bf16[1,512,16,128]{3,1,2,0:T(8,128)(2,1)} %copy-done.4) | copy-start | bytes 6291460
  277.9 4.2 %copy-start.18 = (f32[640,16,8]{0,2,1:T(8,128)S(1)}, f32[640,16,8]{0,2,1:T(8,128)}, u32[]{:S(2)}) copy-start(f32[640,16,8]{0,2,1:T(8,128)} %copy-done.17) | copy-start | bytes 983044
  277.9 4.2 %copy-start.20 = (f32[640,16]{0,1:T(8,128)S(1)}, f32[640,16]{0,1:T(8,128)}, u32[]{:S(2)}) copy-start(f32[640,16]{0,1:T(8,128)} %copy-done.19) | copy-start | bytes 122884
  277.9 4.2 %copy-start.33 = (f32[640]{0:T(1024)S(1)}, f32[640]{0:T(1024)}, u32[]{:S(2)}) copy-start(f32[640]{0:T(1024)} %copy-done.32) | copy-start | bytes 7684
  285.2 104.1 %all-reduce.8.cloned.1.call-start = ((), (), s32[]{:S(2)}) async-start(), calls=%async_computation.1 | async-start | bytes 262144 | tf_op jit(solution)/shard_map/psum | solution.py:15
  (1 other events, 0.8 us)
Sparse Core Ops, SparseCore 0:
  285.3 70.5 all-reduce.5
  358.3 30.9 all-reduce.7
